TPU v7x, 32 devices: a whole 2x2x4 slice. The times are simulated.
32 devices in a mesh: date: 16 (over z, y, x), pix: 2 (over core).
Axes of the slice: x: 2, y: 2, z: 4, core: 2. Of those that a mesh axis runs over, the one named last changes fastest.
Arguments:
- reflect: bfloat16 [64, 6, 16384], P('date', None, 'pix'), may hold values from -8 to 8
- cloud_free: int32 [64, 16384], P('date', 'pix'), may hold values from 0 to 1, as said below
- days: int32 [64], P('date'), may hold values from 1 to 2079, as said below
Outputs:
- median: float32 [6, 16384], P(None, 'pix')
- slope: float32 [6, 16384], P(None, 'pix')
Inputs may be any that keep to these rules, and one draw needn't show every extreme that they name: `cloud_free`: every pixel is clear on at least one of the first 32 dates and on at least one of the others; clear shares differ between tiles. `days`: strictly increasing.
All inputs are finite; a program needn't handle non-finite values.
Results may differ from a plain program's by a relative error of at most 0.0003.
Values may be sent and summed in bfloat16 or wider, within the bound.
A program may use at most 64 MiB of HBM per device.

v0:
```python
import jax
import jax.numpy as jnp
from jax import lax
from jax.sharding import PartitionSpec as P

ridge = 1.0
sentinel = 100.0


def count_ranks(carry, own, piece):

    def step(i, state):
        less, equal, count = state
        other = lax.dynamic_index_in_dim(piece, i, 0, keepdims=True).astype(jnp.float32)
        less = less + (other < own).astype(jnp.float32)
        equal = equal + (other == own).astype(jnp.float32)
        count = count + (other[0, 0] < 50.0).astype(jnp.float32)
        return (less, equal, count)

    return lax.fori_loop(0, piece.shape[0], step, carry)


def select_sums(values, valid, less, equal, count):
    lower = jnp.floor((count - 1.0) / 2.0)
    upper = jnp.floor(count / 2.0)
    low_pick = valid[:, None, :] * ((less <= lower) & (lower < less + equal)).astype(jnp.float32)
    high_pick = valid[:, None, :] * ((less <= upper) & (upper < less + equal)).astype(jnp.float32)
    return (
        jnp.sum(low_pick * values, 0),
        jnp.sum(low_pick, 0),
        jnp.sum(high_pick * values, 0),
        jnp.sum(high_pick, 0),
    )


def finish_median(low_num, low_den, high_num, high_den):
    return 0.5 * (low_num / jnp.maximum(low_den, 1.0) + high_num / jnp.maximum(high_den, 1.0))


def column_median(moved):
    column = moved.astype(jnp.float32)
    column_valid = (column[:, 0, :] < 50.0).astype(jnp.float32)
    zeros = jnp.zeros(column.shape, jnp.float32)
    start_carry = (zeros, zeros, jnp.zeros((column.shape[2],), jnp.float32))
    less, equal, count = count_ranks(start_carry, column, moved)
    low_num, low_den, high_num, high_den = select_sums(column, column_valid, less, equal, count)
    return (column, column_valid, finish_median(low_num, low_den, high_num, high_den))


def fit_slope(s_zero, s_one, s_two, s_y, s_ty):
    first = s_zero + ridge
    determinant = first * (s_two + ridge) - s_one * s_one
    return (first[None, :] * s_ty - s_one[None, :] * s_y) / determinant[None, :]


def local(reflect, cloud_free, days):
    values = reflect.astype(jnp.float32)
    valid = cloud_free.astype(jnp.float32)
    years = days.astype(jnp.float32) / 365.0
    csum = jnp.sum(values * valid[:, None, :], 2)
    cnt = jnp.sum(valid, 1)
    csum, cnt = lax.psum((csum, cnt), "pix")
    scene_mean = csum / jnp.maximum(cnt, 1.0)[:, None]
    marked = jnp.where(valid[:, None, :] > 0, values, sentinel).astype(jnp.bfloat16)
    shifted = values - scene_mean[:, :, None]
    weighted = valid[:, None, :] * shifted
    s_zero = jnp.sum(valid, 0)
    s_one = jnp.sum(years[:, None] * valid, 0)
    s_two = jnp.sum((years * years)[:, None] * valid, 0)
    s_y = jnp.sum(weighted, 0)
    s_ty = jnp.sum(years[:, None, None] * weighted, 0)
    moved = lax.all_to_all(marked, "date", split_axis=2, concat_axis=0, tiled=True)
    column, column_valid, part_median = column_median(moved)
    median = lax.all_gather(part_median, "date", axis=1, tiled=True)
    s_y, s_ty, s_zero, s_one, s_two = lax.psum((s_y, s_ty, s_zero, s_one, s_two), "date")
    slope = fit_slope(s_zero, s_one, s_two, s_y, s_ty)
    return (median, slope)


def solution(mesh):
    placed = (P("date", None, "pix"), P("date", "pix"), P("date"))
    return jax.shard_map(
        local,
        mesh=mesh,
        in_specs=placed,
        out_specs=(P(None, "pix"), P(None, "pix")),
        check_vma=False,
    )
```

profile of v0, /device:TPU:0, one launch (start us, length us, event | category | flops | bytes accessed | tf_op | source)
XLA Modules:
  0.0 414.7 jit_solution(17819752993265104546)
XLA Ops:
  7.9 1.8 convert_reduce_fusion.1
  9.7 0.9 convert_element_type.50
  10.7 1.0 broadcast_compare_fusion
  11.6 1.3 fusion.4
  12.9 2.6 all-reduce.2
  15.6 3.0 fusion.8
  18.6 8.5 %copy.37 = bf16[4,6,8192]{1,0,2:T(4,128)(2,1)} copy(bf16[4,6,8192]{2,0,1:T(4,128)(2,1)S(1)} %get-tuple-element.172) | data formatting | bytes 786432 | tf_op jit(solution)/shard_map/convert_element_type | solution.py:64
  27.2 14.3 %reshape.24 = bf16[16,2,6144]{2,1,0:T(2,128)(2,1)} reshape(bf16[8192,4,6]{2,1,0:T(4,128)(2,1)} %bitcast.17) | data formatting | bytes 786432
  41.5 8.2 %all-to-all-start = ((bf16[16,2,6144]{2,1,0:T(2,128)(2,1)}), bf16[16,2,6144]{2,1,0:T(2,128)(2,1)S(1)}, u32[]{:S(2)}, u32[]{:S(2)}) async-start(bf16[16,2,6144]{2,1,0:T(2,128)(2,1)} %reshape.24), calls=%async_computation | async-start | bytes 786432 | tf_op jit(solution)/shard_map/all_to_all | solution.py:72
  49.7 72.8 %all-reduce.6.cloned.1.call-done = (f32[8192]{0:T(1024)}, f32[8192]{0:T(1024)}, f32[8192]{0:T(1024)}) async-done(((f32[8192]{0:T(1024)}, f32[8192]{0:T(1024)}, f32[8192]{0:T(1024)}), (f32[8192]{0:T(1024)}, f32[8192]{0:T(1024)}, f32[8192]{0:T(1024)})) %all-reduce.6.cloned.1.call-update) | async-done | bytes 98320 | tf_op jit(solution)/shard_map/psum | solution.py:75
  122.5 0.8 broadcast_add_fusion
  123.4 114.3 %all-reduce.8.cloned.1.call-done = (f32[6,8192]{1,0:T(8,128)}, f32[6,8192]{1,0:T(8,128)}) async-done(((f32[6,8192]{1,0:T(8,128)}, f32[6,8192]{1,0:T(8,128)}), (f32[6,8192]{1,0:T(8,128)}, f32[6,8192]{1,0:T(8,128)})) %all-reduce.8.cloned.1.call-update) | async-done | bytes 393232 | tf_op jit(solution)/shard_map/psum | solution.py:75
  237.7 1.8 subtract_divide_fusion
  239.5 20.0 %reshape.25 = bf16[8192,4,6]{2,1,0:T(4,128)(2,1)} reshape(bf16[16,2,6144]{2,1,0:T(2,128)(2,1)S(1)} %all-to-all-done) | data formatting | bytes 786432
  259.5 12.9 %copy.38 = bf16[16,4,6,512]{3,2,1,0:T(8,128)(2,1)} copy(bf16[16,4,6,512]{2,1,3,0:T(4,128)(2,1)} %bitcast.18) | data formatting | bytes 786432 | tf_op jit(solution)/shard_map/all_to_all | solution.py:72
  272.3 1.2 bitcast_convert_fusion
  273.7 91.0 %while.18 = (s32[]{:T(128)}, f32[64,6,512]{2,1,0:T(8,128)S(1)}, f32[64,6,512]{2,1,0:T(8,128)S(1)}, f32[512]{0:T(512)S(1)}, bf16[64,6,512]{2,1,0:T(8,128)(2,1)}, ...) while((s32[]{:T(128)}, f32[64,6,512]{2,1,0:T(8,128)S(1)}, f32[64,6,512]{2,1,0:T(8,128)S(1)}, ...), condition=%wide.region_1.0_spmd.clone, body=%wide.region_0.0_spmd.clone.sunk | while | flops 1577987 | bytes 3985508 | solution.py:20
  273.7 0.7 dynamic-slice_convert_fusion.2
  275.1 0.7 dynamic-slice_convert_fusion.2
  276.5 0.7 dynamic-slice_convert_fusion.2
  277.9 0.7 dynamic-slice_convert_fusion.2
  279.4 0.7 dynamic-slice_convert_fusion.2
  280.8 0.7 dynamic-slice_convert_fusion.2
  282.2 0.7 dynamic-slice_convert_fusion.2
  283.6 0.7 dynamic-slice_convert_fusion.2
  289.3 0.7 dynamic-slice_convert_fusion.2
  290.7 0.7 dynamic-slice_convert_fusion.2
  292.2 0.7 dynamic-slice_convert_fusion.2
  293.6 0.7 dynamic-slice_convert_fusion.2
  295.0 0.7 dynamic-slice_convert_fusion.2
  296.4 0.7 dynamic-slice_convert_fusion.2
  297.9 0.7 dynamic-slice_convert_fusion.2
  299.3 0.7 dynamic-slice_convert_fusion.2
  300.7 0.7 dynamic-slice_convert_fusion.2
  302.1 0.7 dynamic-slice_convert_fusion.2
  303.5 0.7 dynamic-slice_convert_fusion.2
  305.0 0.7 dynamic-slice_convert_fusion.2
  306.4 0.7 dynamic-slice_convert_fusion.2
  307.8 0.7 dynamic-slice_convert_fusion.2
  309.2 0.7 dynamic-slice_convert_fusion.2
  310.6 0.7 dynamic-slice_convert_fusion.2
  316.3 0.7 dynamic-slice_convert_fusion.2
  317.8 0.7 dynamic-slice_convert_fusion.2
  319.2 0.7 dynamic-slice_convert_fusion.2
  320.6 0.7 dynamic-slice_convert_fusion.2
  322.0 0.7 dynamic-slice_convert_fusion.2
  365.1 1.6 fusion.1
  366.8 40.4 %all_gather.3 = f32[6,8192]{1,0:T(8,128)S(1)} all-gather(f32[6,512]{1,0:T(8,128)S(1)} %add_multiply_fusion), channel_id=1, replica_groups=mesh['date'=16,'pix'=2] {'date'}, dimensions={1}, use_global_device_ids=true | all-gather | bytes 208896 | tf_op jit(solution)/shard_map/all_gather | solution.py:74
  (244 shorter events, 70.8 us)
Async XLA Ops:
  7.2 115.4 %all-reduce.6.cloned.1.call-start = ((), (), s32[]{:S(2)}) async-start(), calls=%async_computation.1 | async-start | bytes 196608 | tf_op jit(solution)/shard_map/psum | solution.py:75
  9.7 228.0 %all-reduce.8.cloned.1.call-start = ((), (), s32[]{:S(2)}) async-start(), calls=%async_computation.2 | async-start | bytes 1048576 | tf_op jit(solution)/shard_map/psum | solution.py:75
  41.5 198.0 %all-to-all-start = ((bf16[16,2,6144]{2,1,0:T(2,128)(2,1)}), bf16[16,2,6144]{2,1,0:T(2,128)(2,1)S(1)}, u32[]{:S(2)}, u32[]{:S(2)}) async-start(bf16[16,2,6144]{2,1,0:T(2,128)(2,1)} %reshape.24), calls=%async_computation | async-start | bytes 786432 | tf_op jit(solution)/shard_map/all_to_all | solution.py:72
Sparse Core Ops, SparseCore 0:
  13.8 108.7 all-reduce.5
  128.3 109.3 all-reduce.7
where the time goes:
time: 419 us; the launch traced here: 415 us
  waiting for transfers between devices  187 us (45%)
  other arithmetic  104 us (25%)
  local copies, waits for them, and re-layouts  56.4 us (13%)
  blocking collectives  43 us (10%)
  between operations  14.1 us (3%)
  starting transfers between devices  8.26 us (2%)
    psum x2, waiting for transfers between devices, local(): lax.psum((s_y, s_ty, s_zero, s_one, s_two), 'date')  187 us
    convert_element_type x64, other arithmetic, step(): lax.dynamic_index_in_dim(piece, i, 0, keepdims=True).astype(jnp.float32)  45.1 us
    add x64, other arithmetic, step(): equal = equal + (other == own).astype(jnp.float32)  42.9 us
    all_gather x1, blocking collectives, local(): median = lax.all_gather(part_median, 'date', axis=1, tiled=True)  40.4 us
    unnamed x4, local copies, waits for them, and re-layouts  35 us
    all_to_all x1, local copies, waits for them, and re-layouts, local(): lax.all_to_all(marked, 'date', split_axis=2, concat_axis=0, tiled=True)  12.9 us
    convert_element_type x1, local copies, waits for them, and re-layouts, local(): jnp.where(valid[:, None, :] > 0, values, sentinel).astype(jnp.bfloat16)  8.54 us
  transfers between devices with their start and end apart: 3, of which 2 were waited for; matrix products, arithmetic and copies ran while one was open for 8% of the time, Pallas kernels for 0%

commit v1 on v0

--- a/solution.py
+++ b/solution.py
@@ -69,7 +69,10 @@
     s_two = jnp.sum((years * years)[:, None] * valid, 0)
     s_y = jnp.sum(weighted, 0)
     s_ty = jnp.sum(years[:, None, None] * weighted, 0)
-    moved = lax.all_to_all(marked, "date", split_axis=2, concat_axis=0, tiled=True)
+    moved = jnp.concatenate(
+        lax.all_to_all(jnp.stack(jnp.split(marked, lax.axis_size("date"), axis=2)), "date", 0, 0),
+        axis=0,
+    )
     column, column_valid, part_median = column_median(moved)
     median = lax.all_gather(part_median, "date", axis=1, tiled=True)
     s_y, s_ty, s_zero, s_one, s_two = lax.psum((s_y, s_ty, s_zero, s_one, s_two), "date")

time: 419 us -> 385 us (0.919)
  local copies, waits for them, and re-layouts: 56.4 us -> 11.8 us
  waiting for transfers between devices: 187 us -> 204 us
  other arithmetic: 104 us -> 98.1 us
    unnamed x4 -> x27, local copies, waits for them, and re-layouts: 35 us -> 11.1 us
    psum x2, waiting for transfers between devices: 187 us -> 204 us  [local(): lax.psum((s_y, s_ty, s_zero, s_one, s_two), 'date')]
    all_to_all x1, local copies, waits for them, and re-layouts: 12.9 us -> 0.09 us  [local(): lax.all_to_all(jnp.stack(jnp.split(marked, lax.axis_size('date'), axis=2)...]
    convert_element_type x1 -> x0, local copies, waits for them, and re-layouts: 8.54 us -> none  [local(): jnp.where(valid[:, None, :] > 0, values, sentinel).astype(jnp.bfloat16)]
  transfers between devices with their start and end apart: 3 -> 3, of which waited for: 2 -> 2; matrix products, arithmetic and copies ran while one was open for 8% -> 4% of each run, Pallas kernels for 0% -> 0%
where the time goes in v1:
time: 385 us; the launch traced here: 381 us
  waiting for transfers between devices  204 us (53%)
  other arithmetic  98.1 us (25%)
  blocking collectives  43 us (11%)
  between operations  14.2 us (4%)
  local copies, waits for them, and re-layouts  11.8 us (3%)
  starting transfers between devices  8.26 us (2%)
    psum x2, waiting for transfers between devices, local(): lax.psum((s_y, s_ty, s_zero, s_one, s_two), 'date')  204 us
    convert_element_type x64, other arithmetic, step(): lax.dynamic_index_in_dim(piece, i, 0, keepdims=True).astype(jnp.float32)  45.1 us
    add x64, other arithmetic, step(): equal = equal + (other == own).astype(jnp.float32)  42.9 us
    all_gather x1, blocking collectives, local(): median = lax.all_gather(part_median, 'date', axis=1, tiled=True)  40.4 us
    unnamed x27, local copies, waits for them, and re-layouts  11.1 us
    all_to_all x1, starting transfers between devices, local(): lax.all_to_all(jnp.stack(jnp.split(marked, lax.axis_size('date'), axis=2)...  8.18 us
  transfers between devices with their start and end apart: 3, of which 2 were waited for; matrix products, arithmetic and copies ran while one was open for 4% of the time, Pallas kernels for 0%

profile of v1, /device:TPU:0, one launch (start us, length us, event | category | flops | bytes accessed | tf_op | source)
XLA Modules:
  0.0 380.8 jit_solution(10285455160166653592)
XLA Ops:
  7.2 0.7 fusion.9
  7.9 1.8 convert_reduce_fusion.1
  10.2 2.6 all-reduce.2
  12.9 2.0 fusion.8
  24.7 8.2 %all-to-all-start = ((bf16[16,4,6,512]{3,1,2,0:T(4,128)(2,1)}), bf16[16,4,6,512]{3,1,2,0:T(4,128)(2,1)S(1)}, u32[]{:S(2)}, u32[]{:S(2)}) async-start(bf16[16,4,6,512]{3,1,2,0:T(4,128)(2,1)} %constant_dynamic-update-slice_fusion), calls=%async_computation | async-start | bytes 786432 | tf_op jit(solution)/shard_map/all_to_all | solution.py:73
  32.9 89.7 %all-reduce.6.cloned.1.call-done = (f32[8192]{0:T(1024)}, f32[8192]{0:T(1024)}, f32[8192]{0:T(1024)}) async-done(((f32[8192]{0:T(1024)}, f32[8192]{0:T(1024)}, f32[8192]{0:T(1024)}), (f32[8192]{0:T(1024)}, f32[8192]{0:T(1024)}, f32[8192]{0:T(1024)})) %all-reduce.6.cloned.1.call-update) | async-done | bytes 98320 | tf_op jit(solution)/shard_map/psum | solution.py:78
  122.6 0.8 broadcast_add_fusion
  123.4 114.3 %all-reduce.8.cloned.1.call-done = (f32[6,8192]{1,0:T(8,128)}, f32[6,8192]{1,0:T(8,128)}) async-done(((f32[6,8192]{1,0:T(8,128)}, f32[6,8192]{1,0:T(8,128)}), (f32[6,8192]{1,0:T(8,128)}, f32[6,8192]{1,0:T(8,128)})) %all-reduce.8.cloned.1.call-update) | async-done | bytes 393232 | tf_op jit(solution)/shard_map/psum | solution.py:78
  237.7 1.8 subtract_divide_fusion
  240.6 90.5 %while.18 = (s32[]{:T(128)}, f32[64,6,512]{2,1,0:T(8,128)S(1)}, f32[64,6,512]{2,1,0:T(8,128)S(1)}, f32[512]{0:T(512)S(1)}, bf16[64,6,512]{2,1,0:T(8,128)(2,1)}, ...) while((s32[]{:T(128)}, f32[64,6,512]{2,1,0:T(8,128)S(1)}, f32[64,6,512]{2,1,0:T(8,128)S(1)}, ...), condition=%wide.region_1.0_spmd.clone, body=%wide.region_0.0_spmd.clone.sunk | while | flops 1577987 | bytes 3985516 | solution.py:20
  240.6 0.7 dynamic-slice_convert_fusion.2
  243.4 0.7 dynamic-slice_convert_fusion.2
  244.8 0.7 dynamic-slice_convert_fusion.2
  246.3 0.7 dynamic-slice_convert_fusion.2
  247.7 0.7 dynamic-slice_convert_fusion.2
  249.1 0.7 dynamic-slice_convert_fusion.2
  251.9 0.7 dynamic-slice_convert_fusion.2
  253.3 0.7 dynamic-slice_convert_fusion.2
  254.7 0.7 dynamic-slice_convert_fusion.2
  256.2 0.7 dynamic-slice_convert_fusion.2
  257.6 0.7 dynamic-slice_convert_fusion.2
  260.4 0.7 dynamic-slice_convert_fusion.2
  261.8 0.7 dynamic-slice_convert_fusion.2
  263.2 0.7 dynamic-slice_convert_fusion.2
  264.6 0.7 dynamic-slice_convert_fusion.2
  266.1 0.7 dynamic-slice_convert_fusion.2
  267.5 0.7 dynamic-slice_convert_fusion.2
  270.3 0.7 dynamic-slice_convert_fusion.2
  271.7 0.7 dynamic-slice_convert_fusion.2
  273.1 0.7 dynamic-slice_convert_fusion.2
  274.5 0.7 dynamic-slice_convert_fusion.2
  276.0 0.7 dynamic-slice_convert_fusion.2
  278.8 0.7 dynamic-slice_convert_fusion.2
  280.2 0.7 dynamic-slice_convert_fusion.2
  281.6 0.7 dynamic-slice_convert_fusion.2
  283.0 0.7 dynamic-slice_convert_fusion.2
  284.5 0.7 dynamic-slice_convert_fusion.2
  287.3 0.7 dynamic-slice_convert_fusion.2
  288.7 0.7 dynamic-slice_convert_fusion.2
  290.1 0.7 dynamic-slice_convert_fusion.2
  291.5 0.7 dynamic-slice_convert_fusion.2
  292.9 0.7 dynamic-slice_convert_fusion.2
  294.4 0.7 dynamic-slice_convert_fusion.2
  297.2 0.7 dynamic-slice_convert_fusion.2
  298.6 0.7 dynamic-slice_convert_fusion.2
  300.0 0.7 dynamic-slice_convert_fusion.2
  301.4 0.7 dynamic-slice_convert_fusion.2
  332.8 40.4 %all_gather.3 = f32[6,8192]{1,0:T(8,128)S(1)} all-gather(f32[6,512]{1,0:T(8,128)S(1)} %add_multiply_fusion), channel_id=1, replica_groups=mesh['date'=16,'pix'=2] {'date'}, dimensions={1}, use_global_device_ids=true | all-gather | bytes 208896 | tf_op jit(solution)/shard_map/all_gather | solution.py:77
  (267 shorter events, 76.9 us)
Async XLA Ops:
  7.2 2.7 copy-start.3
  7.2 2.8 copy-start.2
  7.2 115.4 %all-reduce.6.cloned.1.call-start = ((), (), s32[]{:S(2)}) async-start(), calls=%async_computation.1 | async-start | bytes 196608 | tf_op jit(solution)/shard_map/psum | solution.py:78
  9.8 227.9 %all-reduce.8.cloned.1.call-start = ((), (), s32[]{:S(2)}) async-start(), calls=%async_computation.2 | async-start | bytes 1048576 | tf_op jit(solution)/shard_map/psum | solution.py:78
  24.7 214.8 %all-to-all-start = ((bf16[16,4,6,512]{3,1,2,0:T(4,128)(2,1)}), bf16[16,4,6,512]{3,1,2,0:T(4,128)(2,1)S(1)}, u32[]{:S(2)}, u32[]{:S(2)}) async-start(bf16[16,4,6,512]{3,1,2,0:T(4,128)(2,1)} %constant_dynamic-update-slice_fusion), calls=%async_computation | async-start | bytes 786432 | tf_op jit(solution)/shard_map/all_to_all | solution.py:73
  122.6 115.2 %copy-start.4 = (f32[8192]{0:T(1024)S(1)}, f32[8192]{0:T(1024)}, u32[]{:S(2)}) copy-start(f32[8192]{0:T(1024)} %get-tuple-element.159) | copy-start | bytes 98308
  239.6 0.8 copy-start
  331.1 1.0 copy-start.1
Sparse Core Ops, SparseCore 0:
  13.8 108.7 all-reduce.5
  128.3 109.3 all-reduce.7

commit v2 on v0

--- a/solution.py
+++ b/solution.py
@@ -71,7 +71,7 @@
     s_ty = jnp.sum(years[:, None, None] * weighted, 0)
     moved = lax.all_to_all(marked, "date", split_axis=2, concat_axis=0, tiled=True)
     column, column_valid, part_median = column_median(moved)
-    median = lax.all_gather(part_median, "date", axis=1, tiled=True)
+    median = jnp.concatenate(lax.all_gather(part_median, "date"), axis=1)
     s_y, s_ty, s_zero, s_one, s_two = lax.psum((s_y, s_ty, s_zero, s_one, s_two), "date")
     slope = fit_slope(s_zero, s_one, s_two, s_y, s_ty)
     return (median, slope)

time: 419 us -> 419 us (level)
  no operation moved by 1% of the time
where the time goes in v2:
time: 419 us; the launch traced here: 415 us
  waiting for transfers between devices  187 us (45%)
  other arithmetic  104 us (25%)
  local copies, waits for them, and re-layouts  56.4 us (13%)
  blocking collectives  43 us (10%)
  between operations  14.1 us (3%)
  starting transfers between devices  8.26 us (2%)
    psum x2, waiting for transfers between devices, local(): lax.psum((s_y, s_ty, s_zero, s_one, s_two), 'date')  187 us
    convert_element_type x64, other arithmetic, step(): lax.dynamic_index_in_dim(piece, i, 0, keepdims=True).astype(jnp.float32)  45.1 us
    add x64, other arithmetic, step(): equal = equal + (other == own).astype(jnp.float32)  42.9 us
    all_gather x1, blocking collectives, local(): median = jnp.concatenate(lax.all_gather(part_median, 'date'), axis=1)  40.4 us
    unnamed x4, local copies, waits for them, and re-layouts  35 us
    all_to_all x1, local copies, waits for them, and re-layouts, local(): lax.all_to_all(marked, 'date', split_axis=2, concat_axis=0, tiled=True)  12.9 us
    convert_element_type x1, local copies, waits for them, and re-layouts, local(): jnp.where(valid[:, None, :] > 0, values, sentinel).astype(jnp.bfloat16)  8.54 us
  transfers between devices with their start and end apart: 3, of which 2 were waited for; matrix products, arithmetic and copies ran while one was open for 8% of the time, Pallas kernels for 0%

profile of v2, /device:TPU:0, one launch (start us, length us, event | category | flops | bytes accessed | tf_op | source)
XLA Modules:
  0.0 414.7 jit_solution(1926943859644261276)
XLA Ops:
  7.9 1.8 convert_reduce_fusion.1
  9.7 0.9 convert_element_type.50
  10.7 1.0 broadcast_compare_fusion
  11.6 1.3 fusion.4
  12.9 2.6 all-reduce.2
  15.6 3.0 fusion.8
  18.6 8.5 %copy.37 = bf16[4,6,8192]{1,0,2:T(4,128)(2,1)} copy(bf16[4,6,8192]{2,0,1:T(4,128)(2,1)S(1)} %get-tuple-element.172) | data formatting | bytes 786432 | tf_op jit(solution)/shard_map/convert_element_type | solution.py:64
  27.2 14.3 %reshape.79 = bf16[16,2,6144]{2,1,0:T(2,128)(2,1)} reshape(bf16[8192,4,6]{2,1,0:T(4,128)(2,1)} %bitcast.22) | data formatting | bytes 786432
  41.5 8.2 %all-to-all-start = ((bf16[16,2,6144]{2,1,0:T(2,128)(2,1)}), bf16[16,2,6144]{2,1,0:T(2,128)(2,1)S(1)}, u32[]{:S(2)}, u32[]{:S(2)}) async-start(bf16[16,2,6144]{2,1,0:T(2,128)(2,1)} %reshape.79), calls=%async_computation | async-start | bytes 786432 | tf_op jit(solution)/shard_map/all_to_all | solution.py:72
  49.7 72.8 %all-reduce.6.cloned.1.call-done = (f32[8192]{0:T(1024)}, f32[8192]{0:T(1024)}, f32[8192]{0:T(1024)}) async-done(((f32[8192]{0:T(1024)}, f32[8192]{0:T(1024)}, f32[8192]{0:T(1024)}), (f32[8192]{0:T(1024)}, f32[8192]{0:T(1024)}, f32[8192]{0:T(1024)})) %all-reduce.6.cloned.1.call-update) | async-done | bytes 98320 | tf_op jit(solution)/shard_map/psum | solution.py:75
  122.5 0.8 broadcast_add_fusion
  123.4 114.3 %all-reduce.8.cloned.1.call-done = (f32[6,8192]{1,0:T(8,128)}, f32[6,8192]{1,0:T(8,128)}) async-done(((f32[6,8192]{1,0:T(8,128)}, f32[6,8192]{1,0:T(8,128)}), (f32[6,8192]{1,0:T(8,128)}, f32[6,8192]{1,0:T(8,128)})) %all-reduce.8.cloned.1.call-update) | async-done | bytes 393232 | tf_op jit(solution)/shard_map/psum | solution.py:75
  237.7 1.8 subtract_divide_fusion
  239.5 20.0 %reshape.80 = bf16[8192,4,6]{2,1,0:T(4,128)(2,1)} reshape(bf16[16,2,6144]{2,1,0:T(2,128)(2,1)S(1)} %all-to-all-done) | data formatting | bytes 786432
  259.5 12.9 %copy.38 = bf16[16,4,6,512]{3,2,1,0:T(8,128)(2,1)} copy(bf16[16,4,6,512]{2,1,3,0:T(4,128)(2,1)} %bitcast.23) | data formatting | bytes 786432 | tf_op jit(solution)/shard_map/all_to_all | solution.py:72
  272.3 1.2 bitcast_convert_fusion
  273.7 90.9 %while.18 = (s32[]{:T(128)}, f32[64,6,512]{2,1,0:T(8,128)S(1)}, f32[64,6,512]{2,1,0:T(8,128)S(1)}, f32[512]{0:T(512)S(1)}, bf16[64,6,512]{2,1,0:T(8,128)(2,1)}, ...) while((s32[]{:T(128)}, f32[64,6,512]{2,1,0:T(8,128)S(1)}, f32[64,6,512]{2,1,0:T(8,128)S(1)}, ...), condition=%wide.region_1.0_spmd.clone, body=%wide.region_0.0_spmd.clone.sunk | while | flops 1577987 | bytes 3985508 | solution.py:20
  273.7 0.7 dynamic-slice_convert_fusion.2
  275.1 0.7 dynamic-slice_convert_fusion.2
  276.5 0.7 dynamic-slice_convert_fusion.2
  277.9 0.7 dynamic-slice_convert_fusion.2
  280.8 0.7 dynamic-slice_convert_fusion.2
  282.2 0.7 dynamic-slice_convert_fusion.2
  283.6 0.7 dynamic-slice_convert_fusion.2
  285.1 0.7 dynamic-slice_convert_fusion.2
  286.5 0.7 dynamic-slice_convert_fusion.2
  287.9 0.7 dynamic-slice_convert_fusion.2
  289.3 0.7 dynamic-slice_convert_fusion.2
  292.2 0.7 dynamic-slice_convert_fusion.2
  293.6 0.7 dynamic-slice_convert_fusion.2
  296.4 0.7 dynamic-slice_convert_fusion.2
  297.8 0.7 dynamic-slice_convert_fusion.2
  299.3 0.7 dynamic-slice_convert_fusion.2
  300.7 0.7 dynamic-slice_convert_fusion.2
  302.1 0.7 dynamic-slice_convert_fusion.2
  303.5 0.7 dynamic-slice_convert_fusion.2
  304.9 0.7 dynamic-slice_convert_fusion.2
  307.8 0.7 dynamic-slice_convert_fusion.2
  309.2 0.7 dynamic-slice_convert_fusion.2
  310.6 0.7 dynamic-slice_convert_fusion.2
  312.1 0.7 dynamic-slice_convert_fusion.2
  313.5 0.7 dynamic-slice_convert_fusion.2
  314.9 0.7 dynamic-slice_convert_fusion.2
  316.3 0.7 dynamic-slice_convert_fusion.2
  319.2 0.7 dynamic-slice_convert_fusion.2
  320.6 0.7 dynamic-slice_convert_fusion.2
  365.1 1.6 fusion.1
  366.8 40.4 %all-gather.1 = f32[16,6,512]{2,1,0:T(8,128)S(1)} all-gather(f32[1,6,512]{2,1,0:T(8,128)S(1)} %multiply_bitcast_fusion), channel_id=2, replica_groups=mesh['date'=16,'pix'=2] {'date'}, dimensions={0}, use_global_device_ids=true | all-gather | bytes 208896 | tf_op jit(solution)/shard_map/all_gather | solution.py:74
  (244 shorter events, 70.8 us)
Async XLA Ops:
  7.2 115.4 %all-reduce.6.cloned.1.call-start = ((), (), s32[]{:S(2)}) async-start(), calls=%async_computation.1 | async-start | bytes 196608 | tf_op jit(solution)/shard_map/psum | solution.py:75
  9.7 228.0 %all-reduce.8.cloned.1.call-start = ((), (), s32[]{:S(2)}) async-start(), calls=%async_computation.2 | async-start | bytes 1048576 | tf_op jit(solution)/shard_map/psum | solution.py:75
  41.5 198.0 %all-to-all-start = ((bf16[16,2,6144]{2,1,0:T(2,128)(2,1)}), bf16[16,2,6144]{2,1,0:T(2,128)(2,1)S(1)}, u32[]{:S(2)}, u32[]{:S(2)}) async-start(bf16[16,2,6144]{2,1,0:T(2,128)(2,1)} %reshape.79), calls=%async_computation | async-start | bytes 786432 | tf_op jit(solution)/shard_map/all_to_all | solution.py:72
Sparse Core Ops, SparseCore 0:
  13.8 108.7 all-reduce.5
  128.3 109.3 all-reduce.7
